TPU v7x, 256 devices: a whole 4x4x8 slice. The times are simulated.
256 devices in a mesh: row: 32 (over y, z), col: 8 (over x, core).
Axes of the slice: x: 4, y: 4, z: 8, core: 2. Of those that a mesh axis runs over, the one named last changes fastest.
Arguments:
- grams: bfloat16 [4, 3584, 3584], P(None, 'row', 'col'), as said below
- weights: bfloat16 [4, 3584, 7168], P(None, 'row', 'col'), may hold values from -6 to 6
Outputs:
- merged: float32 [3584, 7168], P('row', 'col')
- residual: float32 [3584, 7168], P('row', 'col')
Inputs may be any that keep to these rules, and one draw needn't show every extreme that they name: `grams`: each of the 4 matrices is symmetric and positive definite.
All inputs are finite; a program needn't handle non-finite values.
Results may differ from a plain program's by a relative error of at most 0.012.
The roundings to bfloat16 on the way count: a program that leaves them out, or rounds other values in their place, can miss the bound.
Values may be sent and summed in bfloat16 or wider, within the bound.
A program may use at most 256 MiB of HBM per device.

v0:
```python
import jax
import jax.numpy as jnp
from jax import lax
from jax.sharding import Mesh
from jax.sharding import PartitionSpec as P

ITERS = 2
ROW = ("row_0", "row_1")


def sum_by_axis(so_far, axes):
    for axis in axes:
        so_far = lax.psum_scatter(so_far, axis, scatter_dimension=0, tiled=True)
    return so_far


def sent_to_all(x, axis):
    copies = jnp.broadcast_to(x, (lax.axis_size(axis), *x.shape))
    return lax.all_to_all(copies, axis, split_axis=0, concat_axis=0, tiled=True)


def of_everyone(x, axis):
    return sent_to_all(x, axis).sum(axis=0)


def together(arrays, axis):
    ravelled, at, done = (jnp.concatenate([a.reshape(-1) for a in arrays]), 0, [])
    so_far = of_everyone(ravelled, axis)
    for a in arrays:
        done.append(so_far[at : at + a.size].reshape(a.shape))
        at += a.size
    return tuple(done)


def shards(grams, weights):
    slab_rows = grams.shape[1]
    col_count = weights.shape[2]
    first_row = lax.axis_index(ROW) * slab_rows
    high = lax.Precision.HIGHEST
    gram_slabs = lax.all_gather(grams, "col", axis=2, tiled=True)
    gram_total = jnp.sum(gram_slabs, axis=0, dtype=jnp.float32)
    square_block = lax.dynamic_slice_in_dim(gram_slabs, first_row, slab_rows, gram_slabs.ndim - 1)
    diag_total = jnp.einsum(
        "mr,mrc->rc",
        jnp.diagonal(square_block, axis1=-2, axis2=-1).astype(jnp.float32),
        weights.astype(jnp.float32),
    )
    product = sum_by_axis(
        jnp.einsum("mrk,mrc->kc", gram_slabs, weights, preferred_element_type=jnp.float32), ROW
    )
    right_side = 0.9 * product + 0.1 * diag_total
    total_diag = jnp.diagonal(lax.dynamic_slice_in_dim(gram_total, first_row, slab_rows, 1))
    merged = jnp.zeros((slab_rows, col_count), jnp.float32)
    residual = right_side
    direction = right_side
    for iteration in range(ITERS):
        rounded = direction.astype(jnp.bfloat16)
        shard_piece = lax.all_gather(rounded, ROW, axis=0, tiled=True)
        add_columns = lax.slice_in_dim(gram_total, 0, shard_piece.shape[0], axis=1)
        mapped = jnp.zeros((slab_rows, col_count), jnp.float32) + jnp.dot(
            add_columns, shard_piece.astype(jnp.float32), precision=high
        )
        mapped = 0.9 * mapped + 0.1 * total_diag[:, None] * rounded.astype(jnp.float32)
        curvature, cross_term, square, norm_now = together(
            (
                jnp.sum(direction * mapped, axis=0),
                jnp.sum(residual * mapped, axis=0),
                jnp.sum(mapped * mapped, axis=0),
                jnp.sum(residual * residual, axis=0),
            ),
            ROW,
        )
        step_length = norm_now / curvature
        merged = merged + step_length * direction
        residual = residual - step_length * mapped
        if iteration + 1 < ITERS:
            norm_next = (
                norm_now - 2.0 * step_length * cross_term + step_length * step_length * square
            )
            direction = residual + norm_next / norm_now * direction
    return (merged, residual)


def solution(mesh):
    torus = Mesh(mesh.devices.reshape(4, 8, mesh.shape["col"]), ("row_0", "row_1", "col"))
    in_specs = (P(None, ROW, "col"), P(None, ROW, "col"))
    out_specs = (P(ROW, "col"), P(ROW, "col"))
    return jax.shard_map(
        shards, mesh=torus, in_specs=in_specs, out_specs=out_specs, check_vma=False
    )
```

profile of v0, /device:TPU:32, one launch (start us, length us, event | category | flops | bytes accessed | tf_op | source)
XLA Modules:
  0.0 467.3 jit_solution(11836406161750740182)
XLA Ops:
  7.2 0.0 all-gather.4.cloned.1.call-start
  7.2 2.1 copy.14
  9.3 0.0 all-gather.4.cloned.1.call-update
  9.3 0.0 reduce-scatter.3.cloned.1.call-start
  9.4 35.5 %all-gather.4.cloned.1.call-done = bf16[4,112,3584]{1,2,0:T(8,128)(2,1)} async-done(((bf16[4,112,448]{1,2,0:T(8,128)(2,1)}), bf16[4,112,3584]{1,2,0:T(8,128)(2,1)}) %all-gather.4.cloned.1.call-update) | async-done | bytes 3211280 | tf_op jit(solution)/shard_map/all_gather | solution.py:40
  44.9 8.9 %convolution_bitcast_fusion = f32[3584,896]{1,0:T(8,128)} fusion(bf16[4,112,3584]{1,2,0:T(8,128)(2,1)} %all-gather.4.cloned.1.call-done, bf16[4,112,896]{2,1,0:T(8,128)(2,1)S(1)} %copy-done), kind=kOutput, calls=%fused_computation.2 | convolution fusion | flops 2877292544 | bytes 16859136 | tf_op jit(solution)/shard_map/mrk,mrc->kc/dot_general | solution.py:49
  53.7 0.0 reduce-scatter.3.cloned.1.call-update
  53.8 0.0 reduce-scatter.5.cloned.1.call-start
  53.8 119.3 %reduce-scatter.3.cloned.1.call-done = f32[896,896]{1,0:T(8,128)} async-done(((f32[3584,896]{1,0:T(8,128)}), f32[896,896]{1,0:T(8,128)}) %reduce-scatter.3.cloned.1.call-update) | async-done | bytes 3211280 | tf_op jit(solution)/shard_map/reduce_scatter | solution.py:13
  173.1 0.0 all-gather.6.cloned.1.call-start
  173.2 0.9 constant_dynamic-slice_fusion.1
  174.1 3.2 copy.15
  177.3 2.9 gather_fusion
  180.2 0.6 fusion.2
  180.8 41.3 %reduce-scatter.5.cloned.1.call-done = f32[112,896]{1,0:T(8,128)} async-done(((f32[896,896]{1,0:T(8,128)}), f32[112,896]{1,0:T(8,128)}) %reduce-scatter.5.cloned.1.call-update) | async-done | bytes 401424 | tf_op jit(solution)/shard_map/reduce_scatter | solution.py:13
  222.1 1.8 fusion.10
  223.9 0.0 all-gather.8.cloned.1.call-start
  223.9 3.0 convert_reduce_fusion
  227.0 0.1 copy.24
  227.1 1.7 gather_fusion.1
  228.8 85.2 %all-gather.6.cloned.1.call-done = bf16[3584,896]{1,0:T(8,128)(2,1)} async-done(((bf16[112,896]{1,0:T(8,128)(2,1)}), bf16[3584,896]{1,0:T(8,128)(2,1)}) %all-gather.6.cloned.1.call-update) | async-done | bytes 6422544 | tf_op jit(solution)/shard_map/all_gather | solution.py:58
  314.0 7.0 %multiply_reduce_fusion.6 = (f32[896]{0:T(1024)S(1)}, f32[896]{0:T(1024)S(1)}, f32[896]{0:T(1024)S(1)}, f32[112,896]{1,0:T(8,128)}) fusion(f32[112,896]{1,0:T(8,128)S(1)} %get-tuple-element.14, bf16[112,896]{1,0:T(8,128)(2,1)S(1)} %copy-done.1, f32[112]{0:T(128)S(1)} %broadcast_multiply_fusion, f32[112,3584]{0,1:T(8,128)S(1)} %convert_reduce_fusion, ...), kind=kOutput, calls=%fused_computation.22 | convolution fusion | flops 4316939776 | bytes 9042880 | tf_op jit(solution)/shard_map/dot_general | solution.py:60
  320.9 0.2 broadcast_in_dim.12
  321.2 21.5 %all_to_all.12 = f32[32,1,3584]{2,1,0:T(1,128)S(1)} all-to-all(f32[32,1,3584]{2,1,0:T(1,128)S(1)} %broadcast_in_dim.12), channel_id=1, replica_groups=mesh['row_0'=4,'row_1'=8,'col'=8] {'row_0','row_1'}, dimensions={0} | all-to-all | bytes 917504 | tf_op jit(solution)/shard_map/all_to_all | solution.py:19
  342.7 0.3 reduce_sum.98
  343.0 1.7 fusion.5
  344.8 84.9 %all-gather.8.cloned.1.call-done = bf16[3584,896]{1,0:T(8,128)(2,1)} async-done(((bf16[112,896]{1,0:T(8,128)(2,1)}), bf16[3584,896]{1,0:T(8,128)(2,1)}) %all-gather.8.cloned.1.call-update) | async-done | bytes 6422544 | tf_op jit(solution)/shard_map/all_gather | solution.py:58
  429.7 7.0 %multiply_reduce_fusion.3 = (f32[896]{0:T(1024)S(1)}, f32[896]{0:T(1024)S(1)}, f32[896]{0:T(1024)S(1)}, f32[896]{0:T(1024)S(1)}, f32[112,896]{1,0:T(8,128)}) fusion(f32[112,896]{1,0:T(8,128)S(1)} %get-tuple-element.10, f32[112,896]{1,0:T(8,128)S(1)} %get-tuple-element.14, f32[896]{0:T(1024)S(1)} %get-tuple-element.11, ...), kind=kOutput, calls=%fused_computation.17 | convolution fusion | flops 4317340160 | bytes 9451456 | tf_op jit(solution)/shard_map/dot_general | solution.py:60
  436.7 0.2 broadcast_in_dim.13
  437.0 21.5 %all_to_all.13 = f32[32,1,3584]{2,1,0:T(1,128)S(1)} all-to-all(f32[32,1,3584]{2,1,0:T(1,128)S(1)} %broadcast_in_dim.13), channel_id=1, replica_groups=mesh['row_0'=4,'row_1'=8,'col'=8] {'row_0','row_1'}, dimensions={0} | all-to-all | bytes 917504 | tf_op jit(solution)/shard_map/all_to_all | solution.py:19
  458.5 0.3 reduce_sum.103
  458.8 2.0 multiply_subtract_fusion
  (14 shorter events, 0.1 us)
Async XLA Ops:
  7.2 37.7 %copy-start = (bf16[4,112,896]{2,1,0:T(8,128)(2,1)S(1)}, bf16[4,112,896]{2,1,0:T(8,128)(2,1)}, u32[]{:S(2)}) copy-start(bf16[4,112,896]{2,1,0:T(8,128)(2,1)} %param.3) | copy-start | bytes 2408452
  7.2 37.7 %all-gather.4.cloned.1.call-start = ((), (), s32[]{:S(2)}) async-start(), calls=%async_computation.4 | async-start | bytes 4128768 | tf_op jit(solution)/shard_map/all_gather | solution.py:40
  9.3 163.8 %reduce-scatter.3.cloned.1.call-start = ((), (), s32[]{:S(2)}) async-start(), calls=%async_computation.5 | async-start | bytes 16056320 | tf_op jit(solution)/shard_map/reduce_scatter | solution.py:13
  53.8 168.3 %reduce-scatter.5.cloned.1.call-start = ((), (), s32[]{:S(2)}) async-start(), calls=%async_computation.6 | async-start | bytes 3612672 | tf_op jit(solution)/shard_map/reduce_scatter | solution.py:13
  173.1 140.9 %all-gather.6.cloned.1.call-start = ((), (), s32[]{:S(2)}) async-start(), calls=%async_computation.7 | async-start | bytes 6623232 | tf_op jit(solution)/shard_map/all_gather | solution.py:58
  223.9 90.1 %copy-start.1 = (bf16[112,896]{1,0:T(8,128)(2,1)S(1)}, bf16[112,896]{1,0:T(8,128)(2,1)}, u32[]{:S(2)}) copy-start(bf16[112,896]{1,0:T(8,128)(2,1)} %get-tuple-element.13) | copy-start | bytes 602116
  223.9 205.8 %all-gather.8.cloned.1.call-start = ((), (), s32[]{:S(2)}) async-start(), calls=%async_computation.8 | async-start | bytes 6623232 | tf_op jit(solution)/shard_map/all_gather | solution.py:58
Sparse Core Ops, SparseCore 0:
  9.8 34.9 all-gather.3
  53.9 119.1 reduce-scatter.2
  175.6 46.4 reduce-scatter.4
  225.1 88.8 all-gather.5
  344.9 84.7 all-gather.7
where the time goes:
time: 468 us; the launch traced here: 467 us
  waiting for transfers between devices  366 us (78%)
  blocking collectives  43.1 us (9%)
  matrix products  23.4 us (5%)
  between operations  13.9 us (3%)
  local copies, waits for them, and re-layouts  11.4 us (2%)
  other arithmetic  9.11 us (2%)
    all_gather x2, waiting for transfers between devices, shards(): shard_piece = lax.all_gather(rounded, ROW, axis=0, tiled=True)  170 us
    reduce_scatter x2, waiting for transfers between devices, sum_by_axis(): so_far = lax.psum_scatter(so_far, axis, scatter_dimension=0, tiled=True)  161 us
    all_to_all x2, blocking collectives, sent_to_all(): return lax.all_to_all(copies, axis, split_axis=0, concat_axis=0, tiled=True)  43.1 us
    all_gather x1, waiting for transfers between devices, shards(): gram_slabs = lax.all_gather(grams, 'col', axis=2, tiled=True)  35.5 us
    dot_general x2, matrix products, shards(): jnp.dot(add_columns, shard_piece.astype(jnp.float32), precision=high)  14 us
  transfers between devices with their start and end apart: 5, of which 5 were waited for; matrix products, arithmetic and copies ran while one was open for 3% of the time, Pallas kernels for 0%

commit v1 on v0

--- a/solution.py
+++ b/solution.py
@@ -37,7 +37,7 @@
     col_count = weights.shape[2]
     first_row = lax.axis_index(ROW) * slab_rows
     high = lax.Precision.HIGHEST
-    gram_slabs = lax.all_gather(grams, "col", axis=2, tiled=True)
+    gram_slabs = jnp.concatenate(lax.all_gather(grams, "col"), axis=2)
     gram_total = jnp.sum(gram_slabs, axis=0, dtype=jnp.float32)
     square_block = lax.dynamic_slice_in_dim(gram_slabs, first_row, slab_rows, gram_slabs.ndim - 1)
     diag_total = jnp.einsum(

time: 468 us -> 480 us (1.026)
  local copies, waits for them, and re-layouts: 11.4 us -> 24.4 us
    reshape x0 -> x1, local copies, waits for them, and re-layouts: none -> 7.27 us  [shards(): gram_slabs = jnp.concatenate(lax.all_gather(grams, 'col'), axis=2)]
    all_gather x0 -> x1, local copies, waits for them, and re-layouts: none -> 5.9 us  [shards(): gram_slabs = jnp.concatenate(lax.all_gather(grams, 'col'), axis=2)]
  transfers between devices with their start and end apart: 5 -> 5, of which waited for: 5 -> 5; matrix products, arithmetic and copies ran while one was open for 3% -> 4% of each run, Pallas kernels for 0% -> 0%
where the time goes in v1:
time: 480 us
  waiting for transfers between devices  364 us (76%)
  blocking collectives  43.1 us (9%)
  local copies, waits for them, and re-layouts  24.4 us (5%)
  matrix products  22.7 us (5%)
  between operations  13.9 us (3%)
  other arithmetic  11.7 us (2%)
    all_gather x2, waiting for transfers between devices, shards(): shard_piece = lax.all_gather(rounded, ROW, axis=0, tiled=True)  165 us
    reduce_scatter x2, waiting for transfers between devices, sum_by_axis(): so_far = lax.psum_scatter(so_far, axis, scatter_dimension=0, tiled=True)  161 us
    all_to_all x2, blocking collectives, sent_to_all(): return lax.all_to_all(copies, axis, split_axis=0, concat_axis=0, tiled=True)  43.1 us
    all_gather x1, waiting for transfers between devices, shards(): gram_slabs = jnp.concatenate(lax.all_gather(grams, 'col'), axis=2)  36.9 us
    dot_general x2, matrix products, shards(): jnp.dot(add_columns, shard_piece.astype(jnp.float32), precision=high)  13.3 us
  transfers between devices with their start and end apart: 5, of which 5 were waited for; matrix products, arithmetic and copies ran while one was open for 4% of the time, Pallas kernels for 0%

profile of v1, /device:TPU:32, one launch (start us, length us, event | category | flops | bytes accessed | tf_op | source)
XLA Modules:
  0.0 479.7 jit_solution(3525682709833051854)
XLA Ops:
  7.2 0.7 all-gather.9.cloned.1.call-update
  7.9 0.0 reduce-scatter.3.cloned.1.call-start
  8.0 36.9 %all-gather.9.cloned.1.call-done = bf16[32,112,448]{2,1,0:T(8,128)(2,1)} async-done(((bf16[4,112,448]{2,1,0:T(8,128)(2,1)}), bf16[32,112,448]{2,1,0:T(8,128)(2,1)}) %all-gather.9.cloned.1.call-update) | async-done | bytes 3211280 | tf_op jit(solution)/shard_map/all_gather | solution.py:40
  44.9 5.9 %copy.36 = bf16[8,4,112,448]{3,0,2,1:T(8,128)(2,1)} copy(bf16[8,4,112,448]{3,2,1,0:T(8,128)(2,1)} %bitcast.26) | data formatting | bytes 6422528 | tf_op jit(solution)/shard_map/all_gather | solution.py:40
  50.8 7.3 %reshape.27 = bf16[4,112,3584]{2,1,0:T(8,128)(2,1)} reshape(bf16[4,112,8,448]{3,2,1,0:T(8,128)(2,1)} %bitcast.28) | data formatting | bytes 6422528 | tf_op jit(solution)/shard_map/reshape | solution.py:40
  58.0 8.7 %convolution_bitcast_fusion = f32[3584,896]{1,0:T(8,128)} fusion(bf16[4,112,3584]{2,1,0:T(8,128)(2,1)} %reshape.27, bf16[4,112,896]{2,1,0:T(8,128)(2,1)S(1)} %copy-done), kind=kOutput, calls=%fused_computation.2 | convolution fusion | flops 2877292544 | bytes 16859136 | tf_op jit(solution)/shard_map/mrk,mrc->kc/dot_general | solution.py:49
  66.8 0.0 reduce-scatter.5.cloned.1.call-start
  66.8 119.3 %reduce-scatter.3.cloned.1.call-done = f32[896,896]{1,0:T(8,128)} async-done(((f32[3584,896]{1,0:T(8,128)}), f32[896,896]{1,0:T(8,128)}) %reduce-scatter.3.cloned.1.call-update) | async-done | bytes 3211280 | tf_op jit(solution)/shard_map/reduce_scatter | solution.py:13
  186.1 0.0 all-gather.5.cloned.1.call-start
  186.2 1.1 constant_dynamic-slice_fusion.1
  187.2 3.0 copy.13
  190.2 2.9 gather_fusion
  193.1 0.6 fusion.2
  193.7 41.4 %reduce-scatter.5.cloned.1.call-done = f32[112,896]{1,0:T(8,128)} async-done(((f32[896,896]{1,0:T(8,128)}), f32[112,896]{1,0:T(8,128)}) %reduce-scatter.5.cloned.1.call-update) | async-done | bytes 401424 | tf_op jit(solution)/shard_map/reduce_scatter | solution.py:13
  235.1 1.8 fusion.10
  236.9 0.2 all-gather.7.cloned.1.call-start
  237.1 5.6 %convert_reduce_fusion = f32[112,8,448]{2,1,0:T(8,128)} fusion(bf16[8,4,112,448]{3,2,1,0:T(8,128)(2,1)} %bitcast.27), kind=kLoop, calls=%fused_computation.3 | loop fusion | flops 2809856 | bytes 4816896 | tf_op jit(solution)/shard_map/reduce_sum | solution.py:41
  242.7 2.1 reduce_sum.97
  244.8 0.1 constant_dynamic-slice_fusion
  244.9 1.7 gather_fusion.1
  246.6 80.5 %all-gather.5.cloned.1.call-done = bf16[3584,896]{1,0:T(8,128)(2,1)} async-done(((bf16[112,896]{1,0:T(8,128)(2,1)}), bf16[3584,896]{1,0:T(8,128)(2,1)}) %all-gather.5.cloned.1.call-update) | async-done | bytes 6422544 | tf_op jit(solution)/shard_map/all_gather | solution.py:58
  327.1 6.6 %multiply_reduce_fusion.6 = (f32[896]{0:T(1024)S(1)}, f32[896]{0:T(1024)S(1)}, f32[896]{0:T(1024)S(1)}, f32[112,896]{1,0:T(8,128)}) fusion(f32[112,896]{1,0:T(8,128)S(1)} %get-tuple-element.14, bf16[112,896]{1,0:T(8,128)(2,1)S(1)} %copy-done.1, f32[112]{0:T(128)S(1)} %broadcast_multiply_fusion, f32[112,3584]{1,0:T(8,128)S(1)} %reduce_sum.97, ...), kind=kOutput, calls=%fused_computation.23 | convolution fusion | flops 4316939776 | bytes 9042880 | tf_op jit(solution)/shard_map/dot_general | solution.py:60
  333.7 0.2 broadcast_in_dim.12
  333.9 21.5 %all_to_all.12 = f32[32,1,3584]{2,1,0:T(1,128)S(1)} all-to-all(f32[32,1,3584]{2,1,0:T(1,128)S(1)} %broadcast_in_dim.12), channel_id=1, replica_groups=mesh['row_0'=4,'row_1'=8,'col'=8] {'row_0','row_1'}, dimensions={0} | all-to-all | bytes 917504 | tf_op jit(solution)/shard_map/all_to_all | solution.py:19
  355.5 0.3 reduce_sum.101
  355.8 1.7 fusion.5
  357.5 84.9 %all-gather.7.cloned.1.call-done = bf16[3584,896]{1,0:T(8,128)(2,1)} async-done(((bf16[112,896]{1,0:T(8,128)(2,1)}), bf16[3584,896]{1,0:T(8,128)(2,1)}) %all-gather.7.cloned.1.call-update) | async-done | bytes 6422544 | tf_op jit(solution)/shard_map/all_gather | solution.py:58
  442.4 6.7 %multiply_reduce_fusion.3 = (f32[896]{0:T(1024)S(1)}, f32[896]{0:T(1024)S(1)}, f32[896]{0:T(1024)S(1)}, f32[896]{0:T(1024)S(1)}, f32[112,896]{1,0:T(8,128)}) fusion(f32[112,896]{1,0:T(8,128)S(1)} %get-tuple-element.10, f32[112,896]{1,0:T(8,128)S(1)} %get-tuple-element.14, f32[896]{0:T(1024)S(1)} %get-tuple-element.11, ...), kind=kOutput, calls=%fused_computation.18 | convolution fusion | flops 4317340160 | bytes 9451456 | tf_op jit(solution)/shard_map/dot_general | solution.py:60
  449.1 0.2 broadcast_in_dim.13
  449.4 21.5 %all_to_all.13 = f32[32,1,3584]{2,1,0:T(1,128)S(1)} all-to-all(f32[32,1,3584]{2,1,0:T(1,128)S(1)} %broadcast_in_dim.13), channel_id=1, replica_groups=mesh['row_0'=4,'row_1'=8,'col'=8] {'row_0','row_1'}, dimensions={0} | all-to-all | bytes 917504 | tf_op jit(solution)/shard_map/all_to_all | solution.py:19
  470.9 0.3 reduce_sum.106
  471.2 2.0 multiply_subtract_fusion
  (15 shorter events, 0.2 us)
Async XLA Ops:
  7.2 50.9 %copy-start = (bf16[4,112,896]{2,1,0:T(8,128)(2,1)S(1)}, bf16[4,112,896]{2,1,0:T(8,128)(2,1)}, u32[]{:S(2)}) copy-start(bf16[4,112,896]{2,1,0:T(8,128)(2,1)} %param.3) | copy-start | bytes 2408452
  7.2 37.7 %all-gather.9.cloned.1.call-start = ((), (), s32[]{:S(2)}) async-start(), calls=%async_computation.8 | async-start | bytes 4128768 | tf_op jit(solution)/shard_map/all_gather | solution.py:40
  7.9 178.2 %reduce-scatter.3.cloned.1.call-start = ((), (), s32[]{:S(2)}) async-start(), calls=%async_computation.4 | async-start | bytes 16056320 | tf_op jit(solution)/shard_map/reduce_scatter | solution.py:13
  66.8 168.3 %reduce-scatter.5.cloned.1.call-start = ((), (), s32[]{:S(2)}) async-start(), calls=%async_computation.5 | async-start | bytes 3612672 | tf_op jit(solution)/shard_map/reduce_scatter | solution.py:13
  186.1 140.9 %all-gather.5.cloned.1.call-start = ((), (), s32[]{:S(2)}) async-start(), calls=%async_computation.6 | async-start | bytes 6623232 | tf_op jit(solution)/shard_map/all_gather | solution.py:58
  236.9 205.6 %all-gather.7.cloned.1.call-start = ((), (), s32[]{:S(2)}) async-start(), calls=%async_computation.7 | async-start | bytes 6623232 | tf_op jit(solution)/shard_map/all_gather | solution.py:58
  242.7 84.3 %copy-start.1 = (bf16[112,896]{1,0:T(8,128)(2,1)S(1)}, bf16[112,896]{1,0:T(8,128)(2,1)}, u32[]{:S(2)}) copy-start(bf16[112,896]{1,0:T(8,128)(2,1)} %get-tuple-element.13) | copy-start | bytes 602116
Sparse Core Ops, SparseCore 0:
  9.8 34.9 all-gather.8
  66.9 119.1 reduce-scatter.2
  188.7 46.3 reduce-scatter.4
  238.1 88.9 all-gather.4
  357.7 84.7 all-gather.6
